TPU v7x, 256 devices: a whole 4x4x8 slice. The times are simulated.
256 devices in a mesh: dp: 8 (over x, core), vocab: 32 (over z, y).
Axes of the slice: x: 4, y: 4, z: 8, core: 2. Of those that a mesh axis runs over, the one named last changes fastest.
Arguments:
- hidden: bfloat16 [1024, 8192], P('dp'), may hold values from -600 to 600
- out_weight: bfloat16 [8192, 98304], P('dp', 'vocab'), may hold values from -0.5 to 0.5
- targets: int32 [1024], P('dp'), may hold values from 0 to 98303
- segment: int32 [1024], P('dp'), may hold values from 0 to 31, never falling along the last dimension, each value on 1 to 64 neighbouring positions
- loss_mask: int32 [1024], P('dp'), may hold values 0 or 1
- outside_count: int32 [32], replicated, may hold values from 0 to 3
Outputs:
- token_loss: float32 [1024], P('dp')
- sample_loss: float32 [32], replicated
All inputs are finite; a program needn't handle non-finite values. No bound on the sum of `loss_mask` on one device may be relied on, other than what follows from the above.
Results may differ from a plain program's by a relative error of at most 0.0003.
Values may be sent and summed in bfloat16 or wider, within the bound.
A program may use at most 64 MiB of HBM per device.

v0:
```python
import jax
import jax.numpy as jnp
from jax import lax
from jax.sharding import PartitionSpec as P


def from_everyone(value, axis):
    devices = lax.axis_size(axis)
    return lax.all_to_all(
        jnp.broadcast_to(value[None], (devices, *value.shape)), axis, 0, 0, tiled=True
    )


def collected_together(value, axis):
    leaves = jax.tree.leaves(value)
    order = sorted(range(len(leaves)), key=lambda k: -leaves[k].size)
    width = (1, *leaves[order[0]].shape)[-1]
    lines = [
        jnp.pad(leaves[k].reshape(-1), (0, -leaves[k].size % width)).reshape(-1, width)
        for k in order
    ]
    both, at, found = (from_everyone(jnp.concatenate(lines), axis), 0, {})
    for k, line in zip(order, lines):
        section = both[:, at : at + len(line)].reshape(len(both), -1)
        found[k] = section[:, : leaves[k].size].reshape(-1, *leaves[k].shape)
        at += len(line)
    numbers = iter(range(len(leaves)))
    return jax.tree.map(lambda _: found[next(numbers)], value)


def folded_in_pairs(pieces, combine):
    while len(jax.tree.leaves(pieces)[0]) > 1:
        pieces = jax.vmap(combine)(
            *(jax.tree.map(lambda part: part[side::2], pieces) for side in (0, 1))
        )
    return jax.tree.map(lambda part: part[0], pieces)


def merged_2(value, axis, combine):
    pieces = collected_together(value, axis)
    return folded_in_pairs(pieces, combine)


def taken_together(value, axis):
    everything = from_everyone(value, axis)
    return jnp.sum(everything, axis=0)


def in_one(arrays, axis):
    line, at, finished = (jnp.concatenate([a.reshape(-1) for a in arrays]), 0, [])
    so_far = taken_together(line, axis)
    for a in arrays:
        finished.append(so_far[at : at + a.size].reshape(a.shape))
        at += a.size
    return tuple(finished)


def combine_stats(first, second):
    max_first, sum_first, tgt_first = first
    max_second, sum_second, tgt_second = second
    merged = jnp.maximum(max_first, max_second)
    total = sum_first * jnp.exp(max_first - merged) + sum_second * jnp.exp(max_second - merged)
    return (merged, total, tgt_first + tgt_second)


def sample_terms(losses, seg_ids, mask_ids, samples):
    onehot = (seg_ids[:, None] == jnp.arange(samples, dtype=jnp.int32)[None, :]).astype(jnp.float32)
    weights = mask_ids.astype(jnp.float32)
    loss_sum = jnp.dot(losses * weights, onehot, precision=lax.Precision.HIGHEST)
    count = jnp.dot(weights, onehot, precision=lax.Precision.HIGHEST)
    return (loss_sum, count)


def body(hidden, out_weight, targets, segment, loss_mask, outside_count):
    shard_cols = out_weight.shape[1]
    samples = outside_count.shape[0]
    vocab_base = lax.axis_index("vocab") * shard_cols
    mixed = lax.all_to_all(hidden, "dp", split_axis=1, concat_axis=0, tiled=True)
    logits = lax.psum_scatter(
        jnp.dot(mixed, out_weight, preferred_element_type=jnp.float32),
        "dp",
        scatter_dimension=0,
        tiled=True,
    )
    local_max = jnp.max(logits, axis=1)
    sumexp = jnp.sum(jnp.exp(logits - local_max[:, None]), axis=1)
    column_ids = jnp.arange(shard_cols, dtype=jnp.int32)[None, :] + vocab_base
    picked = jnp.sum(jnp.where(column_ids == targets[:, None], logits, 0.0), axis=1)
    largest, total, target_logit = merged_2((local_max, sumexp, picked), "vocab", combine_stats)
    own_loss = largest + jnp.log(total) - target_logit
    loss_sum, count = sample_terms(own_loss, segment, loss_mask, samples)
    loss_sum, count = in_one((loss_sum, count), "dp")
    denom = jnp.maximum(count + outside_count.astype(jnp.float32), 1.0)
    return (own_loss, loss_sum / denom)


def solution(mesh):
    return jax.shard_map(
        body,
        mesh=mesh,
        in_specs=(P("dp", None), P("dp", "vocab"), P("dp"), P("dp"), P("dp"), P()),
        out_specs=(P("dp"), P()),
        check_vma=False,
    )
```

profile of v0, /device:TPU:1, one launch (start us, length us, event | category | flops | bytes accessed | tf_op | source)
XLA Modules:
  0.0 173.5 jit_solution(4096653923758280930)
XLA Ops:
  7.2 0.0 reduce-scatter.2.cloned.1.call-start
  7.2 4.1 %copy.18 = bf16[128,8192]{0,1:T(8,128)(2,1)} copy(bf16[128,8192]{1,0:T(8,128)(2,1)} %param.6) | data formatting | bytes 4194304 | tf_op args[0]
  11.3 32.9 %all_to_all.30 = bf16[128,8,1024]{0,2,1:T(8,128)(2,1)S(1)} all-to-all(bf16[128,8,1024]{0,2,1:T(8,128)(2,1)} %bitcast.29), channel_id=1, replica_groups=mesh['dp'=8,'vocab'=32] {'dp'}, dimensions={1} | all-to-all | bytes 4194304 | tf_op jit(solution)/shard_map/all_to_all | solution.py:78
  44.2 2.6 %copy.19 = bf16[8,128,1024]{2,1,0:T(8,128)(2,1)} copy(bf16[8,128,1024]{1,2,0:T(8,128)(2,1)S(1)} %bitcast.28) | data formatting | bytes 4194304 | tf_op jit(solution)/shard_map/all_to_all | solution.py:78
  46.8 12.2 %fusion.10 = f32[1024,3072]{1,0:T(8,128)} fusion(bf16[1024,1024]{1,0:T(8,128)(2,1)} %bitcast.30, bf16[1024,3072]{1,0:T(8,128)(2,1)} %param.7), kind=kOutput, calls=%fused_computation.25 | convolution fusion | flops 6442450944 | bytes 20971520 | tf_op jit(solution)/shard_map/dot_general | solution.py:80
  59.0 0.0 copy-start.1
  59.0 0.0 reduce-scatter.2.cloned.1.call-update
  59.0 0.0 copy-start.4
  59.0 0.0 copy-start.5
  59.0 0.0 copy-start.3
  59.0 75.1 %reduce-scatter.2.cloned.1.call-done = f32[128,3072]{1,0:T(8,128)} async-done(((f32[1024,3072]{1,0:T(8,128)}), f32[128,3072]{1,0:T(8,128)}) %reduce-scatter.2.cloned.1.call-update) | async-done | bytes 1572880 | tf_op jit(solution)/shard_map/reduce_scatter | solution.py:79
  134.1 0.0 copy-start
  134.1 1.7 reduce_max.9
  135.8 0.0 copy-done.1
  135.8 0.2 copy-done
  136.0 0.5 exponential_reduce_fusion
  136.5 0.6 broadcast_in_dim.9
  137.2 9.6 %all-to-all-start.1 = ((f32[32,3,128]{2,1,0:T(4,128)}), f32[32,3,128]{2,1,0:T(4,128)S(1)}, u32[]{:S(2)}, u32[]{:S(2)}) async-start(f32[32,3,128]{2,1,0:T(4,128)} %broadcast_in_dim.9), calls=%async_computation.2 | async-start | bytes 131072 | tf_op jit(solution)/shard_map/all_to_all | solution.py:9
  146.7 0.0 copy-done.4
  146.7 0.0 copy-done.5
  146.7 0.2 convolution_bitcast_fusion
  146.9 8.6 %all-to-all-done.1 = f32[32,3,128]{2,1,0:T(4,128)S(1)} async-done(((f32[32,3,128]{2,1,0:T(4,128)}), f32[32,3,128]{2,1,0:T(4,128)S(1)}, u32[]{:S(2)}, u32[]{:S(2)}) %all-to-all-start.1) | async-done | bytes 49184 | tf_op jit(solution)/shard_map/all_to_all | solution.py:9
  156.1 0.0 copy-start.2
  156.1 0.2 convolution_bitcast_fusion.1
  156.3 0.1 pad_maximum_fusion.1
  156.4 9.6 %all_to_all.31 = f32[8,1,64]{2,1,0:T(1,128)S(1)} all-to-all(f32[8,1,64]{2,1,0:T(1,128)S(1)} %broadcast_in_dim.10), channel_id=1, replica_groups=mesh['dp'=8,'vocab'=32] {'dp'}, dimensions={0} | all-to-all | bytes 4096 | tf_op jit(solution)/shard_map/all_to_all | solution.py:9
  166.1 0.0 copy-done.3
  166.1 0.6 maximum_divide_fusion
  166.7 0.0 copy-done.2
  (38 shorter events, 0.5 us)
Async XLA Ops:
  7.2 126.9 %reduce-scatter.2.cloned.1.call-start = ((), (), s32[]{:S(2)}) async-start(), calls=%async_computation.4 | async-start | bytes 14155776 | tf_op jit(solution)/shard_map/reduce_scatter | solution.py:79
  59.0 76.8 %copy-start.1 = (s32[128]{0:T(128)S(1)}, s32[128]{0:T(128)}, u32[]{:S(2)}) copy-start(s32[128]{0:T(128)} %param.8) | copy-start | bytes 1540
  59.0 87.7 %copy-start.4 = (s32[128]{0:T(128)S(1)}, s32[128]{0:T(128)}, u32[]{:S(2)}) copy-start(s32[128]{0:T(128)} %param.9) | copy-start | bytes 1540
  59.0 87.7 %copy-start.5 = (s32[128]{0:T(128)S(1)}, s32[128]{0:T(128)}, u32[]{:S(2)}) copy-start(s32[128]{0:T(128)} %param.10) | copy-start | bytes 1540
  59.0 107.1 %copy-start.3 = (s32[32]{0:T(128)S(1)}, s32[32]{0:T(128)}, u32[]{:S(2)}) copy-start(s32[32]{0:T(128)} %param.11) | copy-start | bytes 388
  134.1 1.9 %copy-start = (f32[128,3072]{1,0:T(8,128)S(1)}, f32[128,3072]{1,0:T(8,128)}, u32[]{:S(2)}) copy-start(f32[128,3072]{1,0:T(8,128)} %reduce-scatter.2.cloned.1.call-done) | copy-start | bytes 4718596
  137.2 18.4 %all-to-all-start.1 = ((f32[32,3,128]{2,1,0:T(4,128)}), f32[32,3,128]{2,1,0:T(4,128)S(1)}, u32[]{:S(2)}, u32[]{:S(2)}) async-start(f32[32,3,128]{2,1,0:T(4,128)} %broadcast_in_dim.9), calls=%async_computation.2 | async-start | bytes 131072 | tf_op jit(solution)/shard_map/all_to_all | solution.py:9
  156.1 10.5 %copy-start.2 = (f32[128]{0:T(128)}, f32[128]{0:T(128)S(1)}, u32[]{:S(2)}) copy-start(f32[128]{0:T(128)S(1)} %subtract_bitcast_fusion) | copy-start | bytes 1540
Sparse Core Ops, SparseCore 0:
  59.1 74.9 reduce-scatter.1
where the time goes:
time: 174 us
  waiting for transfers between devices  83.7 us (48%)
  blocking collectives  42.5 us (24%)
  between operations  14.2 us (8%)
  matrix products  12.5 us (7%)
  starting transfers between devices  9.6 us (6%)
  local copies, waits for them, and re-layouts  7.98 us (5%)
  other arithmetic  3 us (2%)
    reduce_scatter x1, waiting for transfers between devices, body(): lax.psum_scatter(jnp.dot(mixed, out_weight, preferred_element_type=jnp.fl...  75.1 us
    all_to_all x1, blocking collectives, body(): lax.all_to_all(hidden, 'dp', split_axis=1, concat_axis=0, tiled=True)  32.9 us
    dot_general x1, matrix products, body(): jnp.dot(mixed, out_weight, preferred_element_type=jnp.float32)  12.2 us
    all_to_all x1, blocking collectives, from_everyone(): lax.all_to_all(jnp.broadcast_to(value[None], (devices, *value.shape)), ax...  9.63 us
    all_to_all x1, starting transfers between devices, from_everyone(): lax.all_to_all(jnp.broadcast_to(value[None], (devices, *value.shape)), ax...  9.56 us
    all_to_all x1, waiting for transfers between devices, from_everyone(): lax.all_to_all(jnp.broadcast_to(value[None], (devices, *value.shape)), ax...  8.61 us
    unnamed x13, local copies, waits for them, and re-layouts  4.31 us
  transfers between devices with their start and end apart: 2, of which 2 were waited for; matrix products, arithmetic and copies ran while one was open for 0% of the time, Pallas kernels for 0%

commit v1 on v0

v1 whole, which is shorter than its diff:
```python
import functools

import jax
import jax.numpy as jnp
from jax import lax
from jax.experimental import pallas as pl
from jax.experimental.pallas import tpu as pltpu
from jax.sharding import PartitionSpec as P

CORES = 2
NY = 4
SAMPLES_MOST = 128
LOW = -3.0e38


def kernel(
    nx, nz, chunks,
    hid, w, tgt, seg, msk, outside,
    o_tok, o_samp,
    feats, weights, meta_out, meta, sent, got, logits,
    st1_out, st1, st2_out, st2, st3_out, st3,
    loc_sem, w_send, w_recv, own_send, own_recv, meta_send, meta_recv,
    hx_send, hx_recv, hy_send, hy_recv, hd_send, hd_recv,
    ring_send, ring_recv,
    s1_send, s1_recv, s2_send, s2_recv, s3_send, s3_recv,
):
    dp = lax.axis_index("dp")
    vocab = lax.axis_index("vocab")
    x, c = dp // CORES, dp % CORES
    z, y = vocab // NY, vocab % NY
    rows = hid.shape[0]
    depth = w.shape[0]
    chip_feats = CORES * depth
    piece = chip_feats // NY
    width = weights.shape[2]
    half_cols = w.shape[1] // CORES

    def dev(xx, cc, zz, yy):
        return (xx * CORES + cc, zz * NY + yy)

    def remote(src, dst, send, recv, to):
        return pltpu.make_async_remote_copy(
            src_ref=src, dst_ref=dst, send_sem=send, recv_sem=recv,
            device_id=to, device_id_type=pl.DeviceIdType.MESH,
        )

    partner = dev(x, 1 - c, z, y)
    y_up, y_down = dev(x, c, z, (y + 1) % NY), dev(x, c, z, (y + NY - 1) % NY)
    x_up, x_down = dev((x + 1) % nx, c, z, y), dev((x + nx - 1) % nx, c, z, y)
    slot1 = y * CORES + c
    n1 = NY * CORES

    def peer1(j):
        s = (slot1 + j) % n1
        return s, dev(x, s % CORES, z, s // CORES)

    def peer2(j):
        s = (z + j) % nz
        return s, dev(x, c, s, y)

    def peer3(j):
        s = (x + j) % nx
        return s, dev(s, c, z, y)

    my_rows = pl.ds(pl.multiple_of(c * rows, rows), rows)
    his_rows = pl.ds(pl.multiple_of((1 - c) * rows, rows), rows)

    meta_out[...] = jnp.zeros_like(meta_out)
    meta_out[0:1, :] = tgt[...]
    meta_out[1:2, :] = seg[...]
    meta_out[2:3, :] = msk[...]
    meta[c] = meta_out[...]
    own_cols = pl.ds(pl.multiple_of(x * chip_feats, 128), chip_feats)
    local_h = pltpu.make_async_copy(
        hid.at[:, own_cols], feats.at[x, my_rows, :], loc_sem.at[0]
    )
    local_h.start()
    my_depth = pl.ds(pl.multiple_of(c * depth, depth), depth)
    his_depth = pl.ds(pl.multiple_of((1 - c) * depth, depth), depth)
    local_w = []
    for j in range(2 * chunks):
        cols = pl.ds(pl.multiple_of(c * half_cols + j * width, 128), width)
        copy = pltpu.make_async_copy(w.at[:, cols], weights.at[j, my_depth, :], loc_sem.at[1 + j])
        copy.start()
        local_w.append(copy)

    barrier = pltpu.get_barrier_semaphore()
    peers = [peer1(j)[1] for j in range(1, n1)]
    peers += [peer2(j)[1] for j in range(1, nz)]
    peers += [peer3(j)[1] for j in range(1, nx)]
    for p in peers:
        pl.semaphore_signal(barrier, inc=1, device_id=p, device_id_type=pl.DeviceIdType.MESH)
    pl.semaphore_wait(barrier, len(peers))

    order = [2, 1, 3]
    y_cols = pl.ds(pl.multiple_of(y * piece, 128), piece)

    def x_copy(d):
        to = (x + d) % nx
        cols = pl.ds(pl.multiple_of(to * chip_feats + y * piece, 128), piece)
        return remote(
            hid.at[:, cols], feats.at[x, my_rows, y_cols],
            hx_send.at[d - 1], hx_recv.at[d - 1], dev(to, c, z, y),
        )

    def w_copy(j):
        cols = pl.ds(pl.multiple_of((1 - c) * half_cols + j * width, 128), width)
        return remote(w.at[:, cols], weights.at[j, my_depth, :], w_send.at[j], w_recv.at[j], partner)

    for d in order:
        x_copy(d).start()
    for j in range(2 * chunks):
        w_copy(j).start()
    own_copy = remote(hid.at[:, own_cols], feats.at[x, my_rows, :], own_send, own_recv, partner)
    own_copy.start()
    meta_copy = remote(meta_out, meta.at[c], meta_send, meta_recv, partner)
    meta_copy.start()

    def place(s, which, part):
        cols = pl.ds(pl.multiple_of(((y + which) % NY) * piece, 128), piece)
        if part is None:
            return feats.at[s, my_rows, cols]
        half = rows // 2
        at = pl.ds(pl.multiple_of(c * rows + part * half, half), half)
        return feats.at[s, at, cols]

    def y_copy(d, s, i):
        which, part, to = [(0, None, y_up), (0, None, y_down), (NY - 1, 0, y_up), (1, 1, y_down)][i]
        ref = place(s, which, part)
        return remote(ref, ref, hy_send.at[d - 1, i], hy_recv.at[d - 1, i], to)

    def y_arrival(d, s, i):
        which, part = [(NY - 1, None), (1, None), (2, 0), (2, 1)][i]
        ref = place(s, which, part)
        return remote(ref, ref, hy_send.at[d - 1, i], hy_recv.at[d - 1, i], y_up)

    def d_copy(d, s, i):
        which, part = [(0, None), (NY - 1, None), (1, None), (2, 0), (2, 1)][i]
        ref = place(s, which, part)
        return remote(ref, ref, hd_send.at[d - 1, i], hd_recv.at[d - 1, i], partner)

    def source(d):
        return (x + nx - d) % nx

    def begin(d):
        s = source(d)
        x_copy(d).wait_recv()
        y_copy(d, s, 0).start()
        y_copy(d, s, 1).start()
        d_copy(d, s, 0).start()

    def finish(d):
        s = source(d)
        y_arrival(d, s, 0).wait_recv()
        y_copy(d, s, 2).start()
        d_copy(d, s, 1).start()
        y_arrival(d, s, 1).wait_recv()
        y_copy(d, s, 3).start()
        d_copy(d, s, 2).start()
        for i in (2, 3):
            y_arrival(d, s, i).wait_recv()
            d_copy(d, s, i + 1).start()
        for i in range(5):
            d_copy(d, s, i).wait_recv()

    def close(d):
        s = source(d)
        x_copy(d).wait_send()
        for i in range(4):
            y_copy(d, s, i).wait_send()
        for i in range(5):
            d_copy(d, s, i).wait_send()

    def part(block, j):
        return jnp.dot(feats[block], weights[j], preferred_element_type=jnp.float32)

    targets = (x_down, x_up, x_up, x_down, x_down, x_up)

    def message(i, k):
        return remote(sent.at[i, k], got.at[i, k], ring_send.at[i, k], ring_recv.at[i, k], targets[i])

    def put(i, k, value):
        sent[i, k] = value
        message(i, k).start()

    def take(i, k):
        message(i, k).wait_recv()
        return got[i, k]

    up, down, far = (x + 1) % nx, (x + nx - 1) % nx, (x + 2) % nx

    for d in order:
        begin(d)
    finish(2)
    for copy in local_w:
        copy.wait()
    for j in range(2 * chunks):
        w_copy(j).wait_recv()

    def first(k, carry):
        put(0, k, part(far, k))
        put(1, k, part(far, chunks + k))
        return carry

    lax.fori_loop(0, chunks, first, 0)
    finish(1)
    finish(3)

    def direct(k, carry):
        put(2, k, part(up, k))
        put(3, k, part(down, chunks + k))
        return carry

    lax.fori_loop(0, chunks, direct, 0)

    def relay(k, carry):
        own_a = part(down, k)
        put(4, k, own_a + take(0, k))
        own_b = part(up, chunks + k)
        put(5, k, own_b + take(1, k))
        return carry

    lax.fori_loop(0, chunks, relay, 0)

    local_h.wait()
    own_copy.wait_recv()
    meta_copy.wait_recv()

    def own(k, carry):
        logits[k] = part(x, k) + take(2, k)
        logits[chunks + k] = part(x, chunks + k) + take(3, k)
        return carry

    lax.fori_loop(0, chunks, own, 0)

    eye = lax.broadcasted_iota(jnp.int32, (rows, rows), 0) == lax.broadcasted_iota(jnp.int32, (rows, rows), 1)

    def to_column(row):
        return jnp.sum(jnp.where(eye, jnp.broadcast_to(row, (rows, rows)), 0.0), axis=1, keepdims=True)

    def to_row(column):
        return jnp.sum(jnp.where(eye, jnp.broadcast_to(column, (rows, rows)), 0.0), axis=0, keepdims=True)

    base = vocab * w.shape[1] + c * half_cols
    target_column = jnp.concatenate(
        [to_column((meta[i, 0:1, :] - base).astype(jnp.float32)) for i in range(CORES)], axis=0
    ).astype(jnp.int32)
    lane = lax.broadcasted_iota(jnp.int32, (CORES * rows, width), 1)

    def stats(j, value, carry):
        largest, total, picked = carry
        new = jnp.maximum(largest, jnp.max(value, axis=1, keepdims=True))
        total = total * jnp.exp(largest - new) + jnp.sum(jnp.exp(value - new), axis=1, keepdims=True)
        hit = lane == target_column - j * width
        picked = picked + jnp.sum(jnp.where(hit, value, 0.0), axis=1, keepdims=True)
        return new, total, picked

    def last(k, carry):
        carry = stats(k, logits[k] + take(4, k), carry)
        return stats(chunks + k, logits[chunks + k] + take(5, k), carry)

    column = (CORES * rows, 1)
    start = (jnp.full(column, LOW, jnp.float32), jnp.zeros(column, jnp.float32), jnp.zeros(column, jnp.float32))
    found = lax.fori_loop(0, chunks, last, start)

    for kind, value in enumerate(found):
        for i in range(CORES):
            st1_out[2 * kind + i : 2 * kind + i + 1, :] = to_row(value[i * rows : (i + 1) * rows])
    st1_out[6:8, :] = jnp.zeros((2, rows), jnp.float32)

    def exchange(n, me, peer, out, buf, send, recv):
        buf[me] = out[...]
        copies = []
        for j in range(1, n):
            _, to = peer(j)
            copy = remote(out, buf.at[me], send.at[j], recv.at[me], to)
            copy.start()
            copies.append(copy)
        for j in range(1, n):
            s, to = peer(j)
            remote(out, buf.at[s], send.at[j], recv.at[s], to).wait_recv()
        return copies

    def merged(n, buf):
        largest = buf[0, 0:2, :]
        for i in range(1, n):
            largest = jnp.maximum(largest, buf[i, 0:2, :])
        total, picked = jnp.zeros_like(largest), jnp.zeros_like(largest)
        for i in range(n):
            total = total + buf[i, 2:4, :] * jnp.exp(buf[i, 0:2, :] - largest)
            picked = picked + buf[i, 4:6, :]
        return largest, total, picked

    pending = exchange(n1, slot1, peer1, st1_out, st1, s1_send, s1_recv)
    for kind, value in enumerate(merged(n1, st1)):
        st2_out[2 * kind : 2 * kind + 2, :] = value
    st2_out[6:8, :] = jnp.zeros((2, rows), jnp.float32)
    pending += exchange(nz, z, peer2, st2_out, st2, s2_send, s2_recv)
    largest, total, picked = merged(nz, st2)
    loss = largest + jnp.log(total) - picked
    o_tok[...] = jnp.where(c == 0, loss[0:1], loss[1:2])

    ids = lax.broadcasted_iota(jnp.int32, (SAMPLES_MOST, rows), 0)
    sums, counts = jnp.zeros((SAMPLES_MOST, 1), jnp.float32), jnp.zeros((SAMPLES_MOST, 1), jnp.float32)
    for i in range(CORES):
        member = ids == meta[i, 1:2, :]
        weight = meta[i, 2:3, :].astype(jnp.float32)
        sums = sums + jnp.sum(jnp.where(member, weight * loss[i : i + 1], 0.0), axis=1, keepdims=True)
        counts = counts + jnp.sum(jnp.where(member, weight, 0.0), axis=1, keepdims=True)
    st3_out[...] = jnp.zeros_like(st3_out)
    st3_out[0:1, :] = to_row(sums)
    st3_out[1:2, :] = to_row(counts)
    pending += exchange(nx, x, peer3, st3_out, st3, s3_send, s3_recv)
    everything = st3[0]
    for i in range(1, nx):
        everything = everything + st3[i]
    samples = outside.shape[1]
    denom = jnp.maximum(everything[1:2, :samples] + outside[...].astype(jnp.float32), 1.0)
    o_samp[...] = everything[0:1, :samples] / denom

    for copy in pending:
        copy.wait_send()
    for d in order:
        close(d)
    for j in range(2 * chunks):
        w_copy(j).wait_send()
    own_copy.wait_send()
    meta_copy.wait_send()

    def drain(k, carry):
        for i in range(6):
            message(i, k).wait_send()
        return carry

    lax.fori_loop(0, chunks, drain, 0)


def body(nx, nz, hidden, out_weight, targets, segment, loss_mask, outside_count):
    rows, depth = hidden.shape[0], out_weight.shape[0]
    half_cols = out_weight.shape[1] // CORES
    width = min(256, half_cols // 2)
    chunks = half_cols // 2 // width
    f32, dma = jnp.float32, pltpu.SemaphoreType.DMA
    samples = outside_count.shape[0]
    n1 = NY * CORES
    vmem = pl.BlockSpec(memory_space=pltpu.VMEM)
    far = pl.BlockSpec(memory_space=pl.ANY)
    tok, samp = pl.pallas_call(
        functools.partial(kernel, nx, nz, chunks),
        out_shape=(
            jax.ShapeDtypeStruct((1, rows), f32),
            jax.ShapeDtypeStruct((1, samples), f32),
        ),
        in_specs=[far, far, vmem, vmem, vmem, vmem],
        out_specs=(vmem, vmem),
        scratch_shapes=[
            pltpu.VMEM((nx, CORES * rows, CORES * depth), jnp.bfloat16),
            pltpu.VMEM((2 * chunks, CORES * depth, width), jnp.bfloat16),
            pltpu.VMEM((8, rows), jnp.int32),
            pltpu.VMEM((CORES, 8, rows), jnp.int32),
            pltpu.VMEM((6, chunks, CORES * rows, width), f32),
            pltpu.VMEM((6, chunks, CORES * rows, width), f32),
            pltpu.VMEM((2 * chunks, CORES * rows, width), f32),
            pltpu.VMEM((8, rows), f32),
            pltpu.VMEM((n1, 8, rows), f32),
            pltpu.VMEM((8, rows), f32),
            pltpu.VMEM((nz, 8, rows), f32),
            pltpu.VMEM((8, SAMPLES_MOST), f32),
            pltpu.VMEM((nx, 8, SAMPLES_MOST), f32),
            dma((1 + 2 * chunks,)),
            dma((2 * chunks,)), dma((2 * chunks,)),
            dma, dma, dma, dma,
            dma((nx - 1,)), dma((nx - 1,)),
            dma((nx - 1, 4)), dma((nx - 1, 4)),
            dma((nx - 1, 5)), dma((nx - 1, 5)),
            dma((6, chunks)), dma((6, chunks)),
            dma((n1,)), dma((n1,)),
            dma((nz,)), dma((nz,)),
            dma((nx,)), dma((nx,)),
        ],
        compiler_params=pltpu.CompilerParams(collective_id=0, has_side_effects=True),
    )(
        hidden, out_weight, targets[None], segment[None], loss_mask[None], outside_count[None]
    )
    return tok.reshape(rows), samp.reshape(samples)


def solution(mesh):
    nx = mesh.shape["dp"] // CORES
    nz = mesh.shape["vocab"] // NY
    return jax.shard_map(
        functools.partial(body, nx, nz),
        mesh=mesh,
        in_specs=(P("dp", None), P("dp", "vocab"), P("dp"), P("dp"), P("dp"), P()),
        out_specs=(P("dp"), P()),
        check_vma=False,
    )
```

time: 174 us -> 98.7 us (0.57)
  Pallas kernels: 0 us -> 95.7 us
  waiting for transfers between devices: 83.7 us -> 0 us
  blocking collectives: 42.5 us -> 0 us
  between operations: 14.2 us -> 0.64 us
  matrix products: 12.5 us -> 0 us
  starting transfers between devices: 9.6 us -> 0 us
  local copies, waits for them, and re-layouts: 7.98 us -> 2.25 us
  other arithmetic: 3 us -> 0 us
    pallas_call x0 -> x1, Pallas kernels: none -> 95.7 us  [body(): pl.pallas_call(functools.partial(kernel, nx, nz, chunks), out_shape=(jax....]
    reduce_scatter x1 -> x0, waiting for transfers between devices: 75.1 us -> none  [body(): lax.psum_scatter(jnp.dot(mixed, out_weight, preferred_element_type=jnp.fl...]
    all_to_all x2 -> x0, blocking collectives: 42.5 us -> none  [the longest x1 32.9 us: body(): lax.all_to_all(hidden, 'dp', split_axis=1, concat_axis=0, tiled=True)]
    dot_general x3 -> x0, matrix products: 12.5 us -> none  [the longest x1 12.2 us: body(): jnp.dot(mixed, out_weight, preferred_element_type=jnp.float32)]
    all_to_all x1 -> x0, starting transfers between devices: 9.56 us -> none  [from_everyone(): lax.all_to_all(jnp.broadcast_to(value[None], (devices, *value.shape)), ax...]
    all_to_all x1 -> x0, waiting for transfers between devices: 8.61 us -> none  [from_everyone(): lax.all_to_all(jnp.broadcast_to(value[None], (devices, *value.shape)), ax...]
    all_to_all x1 -> x0, local copies, waits for them, and re-layouts: 2.62 us -> none  [body(): lax.all_to_all(hidden, 'dp', split_axis=1, concat_axis=0, tiled=True)]
    unnamed x13 -> x2, local copies, waits for them, and re-layouts: 4.31 us -> 2.25 us
  transfers between devices with their start and end apart: 2 -> 0, of which waited for: 2 -> 0; matrix products, arithmetic and copies ran while one was open for 0% -> 0% of each run, Pallas kernels for 0% -> 0%
where the time goes in v1:
time: 98.7 us; the launch traced here: 98.6 us
  Pallas kernels  95.7 us (97%)
  local copies, waits for them, and re-layouts  2.25 us (2%)
    pallas_call x1, Pallas kernels, body(): pl.pallas_call(functools.partial(kernel, nx, nz, chunks), out_shape=(jax....  95.7 us
    unnamed x2, local copies, waits for them, and re-layouts  2.25 us

profile of v1, /device:TPU:1, one launch (start us, length us, event | category | flops | bytes accessed | tf_op | source)
XLA Modules:
  0.0 98.6 jit_solution(7518066396900580610)
XLA Ops:
  0.6 95.7 %shard_map.77 = (f32[1,128]{1,0:T(1,128)}, f32[1,32]{1,0:T(1,128)}) custom-call(bf16[128,8192]{1,0:T(8,128)(2,1)} %hid.1, bf16[1024,3072]{1,0:T(8,128)(2,1)} %w.1, s32[1,128]{1,0:T(1,128)} %bitcast.6, s32[1,128]{1,0:T(1,128)} %bitcast.7, s32[1,128]{1,0:T(1,128)} %bitcast.8, s32[1,32]{1,0:T(1,128)} %bitcast.9), custom_call_target="tpu_custom_call" | custom-call | tf_op jit(solution)/shard_map/pallas_call | solution.py:348
  96.4 1.1 %copy.10 = f32[128]{0:T(128)} copy(f32[128]{0:T(128)} %bitcast.11) | data formatting | bytes 1024
  97.5 1.1 %copy.11 = f32[32]{0:T(128)} copy(f32[32]{0:T(128)} %bitcast.10) | data formatting | bytes 256

commit v2 on v1

v2 whole, which is shorter than its diff:
```python
import functools

import jax
import jax.numpy as jnp
from jax import lax
from jax.experimental import pallas as pl
from jax.experimental.pallas import tpu as pltpu
from jax.sharding import PartitionSpec as P

CORES = 2
NY = 4
SAMPLES_MOST = 128
LOW = -3.0e38
TOP = 32767.0
BOUND = 2.0e-4


def kernel(nx, nz, chunks, exact, hid, w, tgt, seg, msk, outside, o_tok, o_samp, o_bad, *scratch):
    (
        feats, weights, meta_out, meta, sent, got, logits, passing, steps_out, steps_in, errors,
        st1_out, st1, st2_out, st2, st3_out, st3,
        loc_sem, w_send, w_recv, own_send, own_recv, meta_send, meta_recv,
        xn_send, xn_recv, xf_send, xf_recv, xg_send, xg_recv,
        yo_send, yo_recv, yf_send, yf_recv, dd_send, dd_recv,
        ring_send, ring_recv, step_send, step_recv,
        s1_send, s1_recv, s2_send, s2_recv, s3_send, s3_recv, hello,
    ) = scratch
    dp = lax.axis_index("dp")
    vocab = lax.axis_index("vocab")
    x, c = dp // CORES, dp % CORES
    z, y = vocab // NY, vocab % NY
    rows = hid.shape[0]
    depth = w.shape[0]
    chip_feats = CORES * depth
    piece = chip_feats // NY
    width = weights.shape[2]
    half_cols = w.shape[1] // CORES

    def dev(xx, cc, zz, yy):
        return (xx * CORES + cc, zz * NY + yy)

    def remote(src, dst, send, recv, to):
        return pltpu.make_async_remote_copy(
            src_ref=src, dst_ref=dst, send_sem=send, recv_sem=recv,
            device_id=to, device_id_type=pl.DeviceIdType.MESH,
        )

    partner = dev(x, 1 - c, z, y)
    y_up, y_down = dev(x, c, z, (y + 1) % NY), dev(x, c, z, (y + NY - 1) % NY)
    x_up, x_down = dev((x + 1) % nx, c, z, y), dev((x + nx - 1) % nx, c, z, y)
    z_up, z_down = dev(x, c, (z + 1) % nz, y), dev(x, c, (z + nz - 1) % nz, y)
    slot1 = y * CORES + c
    n1 = NY * CORES

    def peer1(j):
        s = (slot1 + j) % n1
        return s, dev(x, s % CORES, z, s // CORES)

    def peer2(j):
        s = (z + j) % nz
        return s, dev(x, c, s, y)

    def peer3(j):
        s = (x + j) % nx
        return s, dev(s, c, z, y)

    my_rows = pl.ds(pl.multiple_of(c * rows, rows), rows)
    his_rows = pl.ds(pl.multiple_of((1 - c) * rows, rows), rows)

    meta_out[...] = jnp.zeros_like(meta_out)
    meta_out[0:1, :] = tgt[...]
    meta_out[1:2, :] = seg[...]
    meta_out[2:3, :] = msk[...]
    meta[c] = meta_out[...]
    own_cols = pl.ds(pl.multiple_of(x * chip_feats, 128), chip_feats)
    local_h = pltpu.make_async_copy(
        hid.at[:, own_cols], feats.at[x, my_rows, :], loc_sem.at[0]
    )
    local_h.start()
    my_depth = pl.ds(pl.multiple_of(c * depth, depth), depth)
    his_depth = pl.ds(pl.multiple_of((1 - c) * depth, depth), depth)
    local_w = []
    for j in range(2 * chunks):
        cols = pl.ds(pl.multiple_of(c * half_cols + j * width, 128), width)
        copy = pltpu.make_async_copy(w.at[:, cols], weights.at[j, my_depth, :], loc_sem.at[1 + j])
        copy.start()
        local_w.append(copy)

    barrier = pltpu.get_barrier_semaphore()
    def signal(sem, to):
        pl.semaphore_signal(sem, inc=1, device_id=to, device_id_type=pl.DeviceIdType.MESH)

    near = [partner, x_up, x_down, y_up, y_down, z_up, z_down]
    for p in near:
        signal(barrier, p)
    pl.semaphore_wait(barrier, len(near))

    def greet(r):
        signal(hello.at[r, 0], z_up)
        signal(hello.at[r, 1], z_down)

    def greeted(r):
        for side in range(2):
            pl.semaphore_wait(hello.at[r, side], 1)

    greet(0)
    half = rows // 2
    sides = (0, 1)
    x_to, y_to = (x_up, x_down), (y_up, y_down)
    up, down, far = (x + 1) % nx, (x + nx - 1) % nx, (x + 2) % nx
    source = (down, up, far)
    y_cols = pl.ds(pl.multiple_of(y * piece, 128), piece)

    def spot(s, which, h):
        at = pl.ds(pl.multiple_of(c * rows + h * half, half), half)
        cols = pl.ds(pl.multiple_of(((y + which) % NY) * piece, 128), piece)
        return feats.at[s, at, cols]

    def mine(to, h):
        cols = pl.ds(pl.multiple_of(to * chip_feats + y * piece, 128), piece)
        return hid.at[pl.ds(h * half, half), cols]

    def x_near(side, h):
        return remote(
            mine((up, down)[side], h), spot(x, 0, h), xn_send.at[side, h], xn_recv.at[side, h], x_to[side]
        )

    def x_far(side):
        return remote(mine(far, side), passing.at[side], xf_send.at[side], xf_recv.at[side], x_to[side])

    def x_pass(side):
        return remote(
            passing.at[side], spot(source[side], 0, side), xg_send.at[side], xg_recv.at[side], x_to[side]
        )

    def w_copy(j):
        cols = pl.ds(pl.multiple_of((1 - c) * half_cols + j * width, 128), width)
        return remote(w.at[:, cols], weights.at[j, my_depth, :], w_send.at[j], w_recv.at[j], partner)

    def y_own(q, h, side):
        ref = spot(source[q], 0, h)
        return remote(ref, ref, yo_send.at[q, h, side], yo_recv.at[q, h, side], y_to[side])

    def y_pass(q, side):
        ref = spot(source[q], (NY - 1, 1)[side], side)
        return remote(ref, ref, yf_send.at[q, side], yf_recv.at[q, side], y_to[side])

    def across(q, which, h):
        ref = spot(source[q], which, h)
        return remote(ref, ref, dd_send.at[q, which, h], dd_recv.at[q, which, h], partner)

    def landed(ref, send, recv):
        remote(ref, ref, send, recv, partner).wait_recv()

    def begin(q, h):
        for side in sides:
            y_own(q, h, side).start()
        across(q, 0, h).start()

    def middle(q, h):
        for side in sides:
            landed(spot(source[q], (NY - 1, 1)[side], h), yo_send.at[q, h, side], yo_recv.at[q, h, side])
            if side == h:
                y_pass(q, side).start()
            across(q, (NY - 1, 1)[side], h).start()

    def finish(q):
        for side in sides:
            landed(spot(source[q], 2, side), yf_send.at[q, side], yf_recv.at[q, side])
            across(q, 2, side).start()

    def whole(q):
        for which in range(NY):
            for h in sides:
                ref = feats.at[
                    source[q],
                    pl.ds(pl.multiple_of((1 - c) * rows + h * half, half), half),
                    pl.ds(pl.multiple_of(((y + which) % NY) * piece, 128), piece),
                ]
                landed(ref, dd_send.at[q, which, h], dd_recv.at[q, which, h])

    for h in sides:
        for side in sides:
            x_near(side, h).start()
    for side in sides:
        x_far(side).start()
    w_order = [i * chunks + k for k in range(chunks) for i in range(2)]
    for j in w_order:
        w_copy(j).start()
    own_copy = remote(hid.at[:, own_cols], feats.at[x, my_rows, :], own_send, own_recv, partner)
    own_copy.start()
    meta_copy = remote(meta_out, meta.at[c], meta_send, meta_recv, partner)
    meta_copy.start()
    greeted(0)
    greet(1)

    for h in sides:
        for q in sides:
            landed(spot(source[q], 0, h), xn_send.at[q, h], xn_recv.at[q, h])
            begin(q, h)
    for side in sides:
        x_far(side).wait_recv()
        x_pass(side).start()
    greeted(1)
    greet(2)
    for h in sides:
        for q in sides:
            middle(q, h)
    for side in sides:
        landed(spot(far, 0, side), xg_send.at[side], xg_recv.at[side])
        begin(2, side)
    for q in sides:
        finish(q)
    for q in sides:
        whole(q)
    for copy in local_w:
        copy.wait()
    for j in range(2 * chunks):
        w_copy(j).wait_recv()
    greeted(2)

    def part(block, j):
        return jnp.dot(feats[block], weights[j], preferred_element_type=jnp.float32)

    targets = (x_down, x_up, x_up, x_down, x_down, x_up)

    def message(i, k):
        return remote(sent.at[i, k], got.at[i, k], ring_send.at[i, k], ring_recv.at[i, k], targets[i])

    def message_steps(i, k):
        return remote(
            steps_out.at[i, k], steps_in.at[i, k], step_send.at[i, k], step_recv.at[i, k], targets[i]
        )

    def put(i, k, value, error=None):
        if exact:
            sent[i, k] = value
            message(i, k).start()
            return
        peak = jnp.max(jnp.abs(value), axis=0, keepdims=True)
        step = jnp.maximum(peak, 1.0e-30) * (1.0 / TOP)
        sent[i, k] = jnp.round(value * (1.0 / step)).astype(jnp.int32).astype(jnp.int16)
        own_error = step * 0.51
        steps_out[i, k] = jnp.concatenate([step, own_error if error is None else own_error + error], axis=0)
        message(i, k).start()
        message_steps(i, k).start()

    def take(i, k):
        message(i, k).wait_recv()
        if exact:
            return got[i, k], None
        message_steps(i, k).wait_recv()
        both = steps_in[i, k]
        return got[i, k].astype(jnp.int32).astype(jnp.float32) * both[0:1], both[1:2]

    def direct(k, carry):
        put(2, k, part(up, k))
        put(3, k, part(down, chunks + k))
        return carry

    lax.fori_loop(0, chunks, direct, 0)
    for h in sides:
        middle(2, h)
    finish(2)
    whole(2)

    def first(k, carry):
        put(0, k, part(far, k))
        put(1, k, part(far, chunks + k))
        return carry

    lax.fori_loop(0, chunks, first, 0)

    def relay(k, carry):
        for i, block in ((0, down), (1, up)):
            mine_too = part(block, i * chunks + k)
            value, error = take(i, k)
            put(4 + i, k, mine_too + value, error)
        return carry

    lax.fori_loop(0, chunks, relay, 0)

    local_h.wait()
    own_copy.wait_recv()
    meta_copy.wait_recv()

    def own(k, carry):
        for i in range(2):
            mine_too = part(x, i * chunks + k)
            value, error = take(2 + i, k)
            logits[i * chunks + k] = mine_too + value
            if not exact:
                errors[i * chunks + k] = error
        return carry

    lax.fori_loop(0, chunks, own, 0)

    eye = lax.broadcasted_iota(jnp.int32, (rows, rows), 0) == lax.broadcasted_iota(jnp.int32, (rows, rows), 1)

    def to_column(row):
        return jnp.sum(jnp.where(eye, jnp.broadcast_to(row, (rows, rows)), 0.0), axis=1, keepdims=True)

    def to_row(column):
        return jnp.sum(jnp.where(eye, jnp.broadcast_to(column, (rows, rows)), 0.0), axis=0, keepdims=True)

    base = vocab * w.shape[1] + c * half_cols
    target_column = jnp.concatenate(
        [to_column((meta[i, 0:1, :] - base).astype(jnp.float32)) for i in range(CORES)], axis=0
    ).astype(jnp.int32)
    lane = lax.broadcasted_iota(jnp.int32, (CORES * rows, width), 1)

    def stats(j, value, carry):
        largest, total, picked = carry
        new = jnp.maximum(largest, jnp.max(value, axis=1, keepdims=True))
        total = total * jnp.exp(largest - new) + jnp.sum(jnp.exp(value - new), axis=1, keepdims=True)
        hit = lane == target_column - j * width
        picked = picked + jnp.sum(jnp.where(hit, value, 0.0), axis=1, keepdims=True)
        return new, total, picked

    def last(k, carry):
        found, worst = carry
        for i in range(2):
            j = i * chunks + k
            value, error = take(4 + i, k)
            found = stats(j, logits[j] + value, found)
            if not exact:
                worst = jnp.maximum(worst, errors[j] + error)
        return found, worst

    column = (CORES * rows, 1)
    zero = jnp.zeros(column, jnp.float32)
    start = (jnp.full(column, LOW, jnp.float32), zero, zero), jnp.zeros((1, width), jnp.float32)
    found, worst = lax.fori_loop(0, chunks, last, start)

    for kind, value in enumerate(found):
        for i in range(CORES):
            st1_out[2 * kind + i : 2 * kind + i + 1, :] = to_row(value[i * rows : (i + 1) * rows])
    st1_out[6:8, :] = jnp.broadcast_to(jnp.max(worst, axis=1, keepdims=True), (2, rows))

    def exchange(n, me, peer, out, buf, send, recv):
        buf[me] = out[...]
        copies = []
        for j in range(1, n):
            _, to = peer(j)
            copy = remote(out, buf.at[me], send.at[j], recv.at[me], to)
            copy.start()
            copies.append(copy)
        for j in range(1, n):
            s, to = peer(j)
            remote(out, buf.at[s], send.at[j], recv.at[s], to).wait_recv()
        return copies

    def merged(n, buf):
        largest = buf[0, 0:2, :]
        for i in range(1, n):
            largest = jnp.maximum(largest, buf[i, 0:2, :])
        total, picked = jnp.zeros_like(largest), jnp.zeros_like(largest)
        for i in range(n):
            total = total + buf[i, 2:4, :] * jnp.exp(buf[i, 0:2, :] - largest)
            picked = picked + buf[i, 4:6, :]
        worst = buf[0, 6:8, :]
        for i in range(1, n):
            worst = jnp.maximum(worst, buf[i, 6:8, :])
        return largest, total, picked, worst

    pending = exchange(n1, slot1, peer1, st1_out, st1, s1_send, s1_recv)
    for kind, value in enumerate(merged(n1, st1)):
        st2_out[2 * kind : 2 * kind + 2, :] = value
    pending += exchange(nz, z, peer2, st2_out, st2, s2_send, s2_recv)
    largest, total, picked, worst = merged(nz, st2)
    loss = largest + jnp.log(total) - picked
    o_tok[...] = jnp.where(c == 0, loss[0:1], loss[1:2])

    ids = lax.broadcasted_iota(jnp.int32, (SAMPLES_MOST, rows), 0)
    sums, counts = jnp.zeros((SAMPLES_MOST, 1), jnp.float32), jnp.zeros((SAMPLES_MOST, 1), jnp.float32)
    for i in range(CORES):
        member = ids == meta[i, 1:2, :]
        weight = meta[i, 2:3, :].astype(jnp.float32)
        sums = sums + jnp.sum(jnp.where(member, weight * loss[i : i + 1], 0.0), axis=1, keepdims=True)
        counts = counts + jnp.sum(jnp.where(member, weight, 0.0), axis=1, keepdims=True)
    st3_out[...] = jnp.zeros_like(st3_out)
    st3_out[0:1, :] = to_row(sums)
    st3_out[1:2, :] = to_row(counts)
    norm = jnp.sum(loss * loss, axis=1, keepdims=True)
    limit = rows * (2.0 * worst[:, 0:1]) ** 2
    bad = jnp.max(jnp.where(limit <= BOUND**2 * norm, 0.0, 1.0), axis=0, keepdims=True)
    st3_out[2:3, :] = jnp.broadcast_to(bad, (1, SAMPLES_MOST))
    st3_out[3:4, :] = worst[0:1]
    pending += exchange(nx, x, peer3, st3_out, st3, s3_send, s3_recv)
    everything, most = st3[0], st3[0]
    for i in range(1, nx):
        everything = everything + st3[i]
        most = jnp.maximum(most, st3[i])
    samples = outside.shape[1]
    count = everything[1:2, :samples]
    denom = jnp.maximum(count + outside[...].astype(jnp.float32), 1.0)
    sample_loss = everything[0:1, :samples] / denom
    o_samp[...] = sample_loss
    off = 2.0 * most[3:4, :samples] * count / denom
    fine = jnp.sum(off * off, axis=1, keepdims=True) <= BOUND**2 * jnp.sum(
        sample_loss * sample_loss, axis=1, keepdims=True
    )
    o_bad[...] = jnp.maximum(most[2:3, :], jnp.where(fine, 0.0, 1.0))

    for copy in pending:
        copy.wait_send()
    for side in sides:
        x_far(side).wait_send()
        x_pass(side).wait_send()
        for h in sides:
            x_near(side, h).wait_send()
    for q in range(3):
        for side in sides:
            y_pass(q, side).wait_send()
            for h in sides:
                y_own(q, h, side).wait_send()
        for which in range(NY):
            for h in sides:
                across(q, which, h).wait_send()
    for j in range(2 * chunks):
        w_copy(j).wait_send()
    own_copy.wait_send()
    meta_copy.wait_send()

    def drain(k, carry):
        for i in range(6):
            message(i, k).wait_send()
            if not exact:
                message_steps(i, k).wait_send()
        return carry

    lax.fori_loop(0, chunks, drain, 0)


def run(nx, nz, exact, hidden, out_weight, targets, segment, loss_mask, outside_count):
    rows, depth = hidden.shape[0], out_weight.shape[0]
    half_cols = out_weight.shape[1] // CORES
    width = min(256, half_cols // 2)
    chunks = half_cols // 2 // width
    f32, dma = jnp.float32, pltpu.SemaphoreType.DMA
    coded = f32 if exact else jnp.int16
    samples = outside_count.shape[0]
    n1 = NY * CORES
    vmem = pl.BlockSpec(memory_space=pltpu.VMEM)
    anywhere = pl.BlockSpec(memory_space=pl.ANY)
    pairs = []
    for shape in [(2, 2), (2,), (2,), (3, 2, 2), (3, 2), (3, NY, 2), (6, chunks), (6, chunks), (n1,), (nz,), (nx,)]:
        pairs += [dma(shape), dma(shape)]
    return pl.pallas_call(
        functools.partial(kernel, nx, nz, chunks, exact),
        out_shape=(
            jax.ShapeDtypeStruct((1, rows), f32),
            jax.ShapeDtypeStruct((1, samples), f32),
            jax.ShapeDtypeStruct((1, SAMPLES_MOST), f32),
        ),
        in_specs=[anywhere, anywhere, vmem, vmem, vmem, vmem],
        out_specs=(vmem, vmem, vmem),
        scratch_shapes=[
            pltpu.VMEM((nx, CORES * rows, CORES * depth), jnp.bfloat16),
            pltpu.VMEM((2 * chunks, CORES * depth, width), jnp.bfloat16),
            pltpu.VMEM((8, rows), jnp.int32),
            pltpu.VMEM((CORES, 8, rows), jnp.int32),
            pltpu.VMEM((6, chunks, CORES * rows, width), coded),
            pltpu.VMEM((6, chunks, CORES * rows, width), coded),
            pltpu.VMEM((2 * chunks, CORES * rows, width), f32),
            pltpu.VMEM((2, rows // 2, CORES * depth // NY), jnp.bfloat16),
            pltpu.VMEM((6, chunks, 2, width), f32),
            pltpu.VMEM((6, chunks, 2, width), f32),
            pltpu.VMEM((2 * chunks, 1, width), f32),
            pltpu.VMEM((8, rows), f32),
            pltpu.VMEM((n1, 8, rows), f32),
            pltpu.VMEM((8, rows), f32),
            pltpu.VMEM((nz, 8, rows), f32),
            pltpu.VMEM((8, SAMPLES_MOST), f32),
            pltpu.VMEM((nx, 8, SAMPLES_MOST), f32),
            dma((1 + 2 * chunks,)),
            dma((2 * chunks,)), dma((2 * chunks,)),
            dma, dma, dma, dma,
            *pairs,
            pltpu.SemaphoreType.REGULAR((3, 2)),
        ],
        compiler_params=pltpu.CompilerParams(collective_id=int(exact), has_side_effects=True),
    )(
        hidden, out_weight, targets[None], segment[None], loss_mask[None], outside_count[None]
    )


def body(nx, nz, *arrays):
    tok, samp, bad = run(nx, nz, False, *arrays)
    tok, samp = lax.cond(
        bad[0, 0] > 0.0,
        lambda *_: run(nx, nz, True, *arrays)[:2],
        lambda *found: found,
        tok, samp,
    )
    return tok.reshape(-1), samp.reshape(-1)


def solution(mesh):
    nx = mesh.shape["dp"] // CORES
    nz = mesh.shape["vocab"] // NY
    return jax.shard_map(
        functools.partial(body, nx, nz),
        mesh=mesh,
        in_specs=(P("dp", None), P("dp", "vocab"), P("dp"), P("dp"), P("dp"), P()),
        out_specs=(P("dp"), P()),
        check_vma=False,
    )
```

time: 98.7 us -> 163 us (1.65)
  Pallas kernels: 95.7 us -> 160 us
    pallas_call x1 -> x2, Pallas kernels: 95.7 us -> 160 us  [run(): pl.pallas_call(functools.partial(kernel, nx, nz, chunks, exact), out_shap...]
where the time goes in v2:
time: 163 us
  Pallas kernels  160 us (98%)
    pallas_call x2, Pallas kernels, run(): pl.pallas_call(functools.partial(kernel, nx, nz, chunks, exact), out_shap...  160 us

profile of v2, /device:TPU:1, one launch (start us, length us, event | category | flops | bytes accessed | tf_op | source)
XLA Modules:
  0.0 162.7 jit_solution(17337298148346464572)
XLA Ops:
  0.6 0.0 copy-start.4
  0.6 0.0 copy-start.3
  0.7 0.0 copy-start.2
  0.7 0.0 copy-start.1
  0.7 0.0 copy-start
  0.7 70.9 %shard_map.77 = (f32[1,128]{1,0:T(1,128)S(1)}, f32[1,32]{1,0:T(1,128)S(1)}, f32[1,128]{1,0:T(1,128)}) custom-call(bf16[128,8192]{1,0:T(8,128)(2,1)} %hid.1, bf16[1024,3072]{1,0:T(8,128)(2,1)} %w.1, s32[1,128]{1,0:T(1,128)} %bitcast.14, s32[1,128]{1,0:T(1,128)} %bitcast.16, s32[1,128]{1,0:T(1,128)} %bitcast.18, s32[1,32]{1,0:T(1,128)} %bitcast.20), custom_call_target="tpu_custom_call" | custom-call | tf_op jit(solution)/shard_map/pallas_call | solution.py:449
  72.2 0.0 copy-done.4
  72.2 0.0 copy-done.3
  72.2 0.0 copy-done.2
  72.3 0.0 copy-done.1
  72.3 0.0 copy-done
  72.3 89.3 %conditional.1 = (f32[128]{0:T(128)S(1)}, f32[32]{0:T(128)S(1)}) conditional(s32[]{:T(128)} %bitcast.12, (f32[1,128]{1,0:T(1,128)S(1)}, f32[1,32]{1,0:T(1,128)S(1)}) %tuple.30, (s32[128]{0:T(128)S(1)}, s32[128]{0:T(128)S(1)}, s32[128]{0:T(128)S(1)}, s32[32]{0:T(128)S(1)}, bf16[128,8192]{1,0:T(8,128)(2,1)S(1)}, ...), branch_computations={%region_0.0_spmd, %region_1.0_spmd} | conditional | bytes 16 | solution.py:490
  72.3 89.3 %branch_1_fun.1 = (f32[1,128]{1,0:T(1,128)S(1)}, f32[1,32]{1,0:T(1,128)S(1)}, f32[1,128]{1,0:T(1,128)}) custom-call(bf16[128,8192]{1,0:T(8,128)(2,1)S(1)} %get-tuple-element.22.hid, bf16[1024,3072]{1,0:T(8,128)(2,1)} %get-tuple-element.23.w, s32[1,128]{1,0:T(1,128)S(1)} %bitcast.15, s32[1,128]{1,0:T(1,128)S(1)} %bitcast.17, s32[1,128]{1,0:T(1,128)S(1)} %bitcast.19, ...), custom_call_target="tpu_custom_call" | custom-call | tf_op jit(solution)/shard_map/cond/branch_1_fun/pallas_call | solution.py:449
  161.6 0.5 copy.16
  162.1 0.5 copy.17
Async XLA Ops:
  0.6 71.6 %copy-start.4 = (s32[32]{0:T(128)S(1)}, s32[32]{0:T(128)}, u32[]{:S(2)}) copy-start(s32[32]{0:T(128)} %param.13) | copy-start | bytes 388
  0.6 71.6 %copy-start.3 = (s32[128]{0:T(128)S(1)}, s32[128]{0:T(128)}, u32[]{:S(2)}) copy-start(s32[128]{0:T(128)} %param.12) | copy-start | bytes 1540
  0.7 71.6 %copy-start.2 = (s32[128]{0:T(128)S(1)}, s32[128]{0:T(128)}, u32[]{:S(2)}) copy-start(s32[128]{0:T(128)} %param.11) | copy-start | bytes 1540
  0.7 71.6 %copy-start.1 = (s32[128]{0:T(128)S(1)}, s32[128]{0:T(128)}, u32[]{:S(2)}) copy-start(s32[128]{0:T(128)} %param.10) | copy-start | bytes 1540
  0.7 71.6 %copy-start = (bf16[128,8192]{1,0:T(8,128)(2,1)S(1)}, bf16[128,8192]{1,0:T(8,128)(2,1)}, u32[]{:S(2)}) copy-start(bf16[128,8192]{1,0:T(8,128)(2,1)} %hid.1) | copy-start | bytes 6291460

commit v3 on v2

--- a/solution.py
+++ b/solution.py
@@ -106,47 +106,50 @@
     greet(0)
     half = rows // 2
     sides = (0, 1)
-    x_to, y_to = (x_up, x_down), (y_up, y_down)
+    x_to, y_to, z_to = (x_up, x_down), (y_up, y_down), (z_up, z_down)
     up, down, far = (x + 1) % nx, (x + nx - 1) % nx, (x + 2) % nx
     source = (down, up, far)
-    y_cols = pl.ds(pl.multiple_of(y * piece, 128), piece)
-
-    def spot(s, which, h):
+    label = ((y + 2 * z) % NY, (z + 2 * y) % NY, (y + 2 * z) % NY)
+    beside = (y_to, z_to, y_to)
+    across_to = (z_to, y_to, z_to)
+
+    def spot(s, q, which, h):
         at = pl.ds(pl.multiple_of(c * rows + h * half, half), half)
-        cols = pl.ds(pl.multiple_of(((y + which) % NY) * piece, 128), piece)
+        cols = pl.ds(pl.multiple_of(((label[q] + which) % NY) * piece, 128), piece)
         return feats.at[s, at, cols]
 
-    def mine(to, h):
-        cols = pl.ds(pl.multiple_of(to * chip_feats + y * piece, 128), piece)
+    def mine(to, q, h):
+        cols = pl.ds(pl.multiple_of(to * chip_feats + label[q] * piece, 128), piece)
         return hid.at[pl.ds(h * half, half), cols]
 
     def x_near(side, h):
         return remote(
-            mine((up, down)[side], h), spot(x, 0, h), xn_send.at[side, h], xn_recv.at[side, h], x_to[side]
+            mine((up, down)[side], side, h), spot(x, side, 0, h),
+            xn_send.at[side, h], xn_recv.at[side, h], x_to[side],
         )
 
     def x_far(side):
-        return remote(mine(far, side), passing.at[side], xf_send.at[side], xf_recv.at[side], x_to[side])
+        return remote(mine(far, 2, side), passing.at[side], xf_send.at[side], xf_recv.at[side], x_to[side])
 
     def x_pass(side):
         return remote(
-            passing.at[side], spot(source[side], 0, side), xg_send.at[side], xg_recv.at[side], x_to[side]
+            passing.at[side], spot(source[side], 2, 0, side), xg_send.at[side], xg_recv.at[side], x_to[side]
         )
 
     def w_copy(j):
         cols = pl.ds(pl.multiple_of((1 - c) * half_cols + j * width, 128), width)
         return remote(w.at[:, cols], weights.at[j, my_depth, :], w_send.at[j], w_recv.at[j], partner)
 
-    def y_own(q, h, side):
-        ref = spot(source[q], 0, h)
-        return remote(ref, ref, yo_send.at[q, h, side], yo_recv.at[q, h, side], y_to[side])
-
-    def y_pass(q, side):
-        ref = spot(source[q], (NY - 1, 1)[side], side)
-        return remote(ref, ref, yf_send.at[q, side], yf_recv.at[q, side], y_to[side])
+    def one(q, h, side):
+        ref = spot(source[q], q, 0, h)
+        return remote(ref, ref, yo_send.at[q, h, side], yo_recv.at[q, h, side], beside[q][side])
+
+    def two(q, side):
+        ref = spot(source[q], q, 0, side)
+        return remote(ref, ref, yf_send.at[q, side], yf_recv.at[q, side], across_to[q][side])
 
     def across(q, which, h):
-        ref = spot(source[q], which, h)
+        ref = spot(source[q], q, which, h)
         return remote(ref, ref, dd_send.at[q, which, h], dd_recv.at[q, which, h], partner)
 
     def landed(ref, send, recv):
@@ -154,20 +157,17 @@
 
     def begin(q, h):
         for side in sides:
-            y_own(q, h, side).start()
+            one(q, h, side).start()
+        two(q, h).start()
         across(q, 0, h).start()
 
     def middle(q, h):
         for side in sides:
-            landed(spot(source[q], (NY - 1, 1)[side], h), yo_send.at[q, h, side], yo_recv.at[q, h, side])
-            if side == h:
-                y_pass(q, side).start()
-            across(q, (NY - 1, 1)[side], h).start()
-
-    def finish(q):
-        for side in sides:
-            landed(spot(source[q], 2, side), yf_send.at[q, side], yf_recv.at[q, side])
-            across(q, 2, side).start()
+            which = (NY - 1, 1)[side]
+            landed(spot(source[q], q, which, h), yo_send.at[q, h, side], yo_recv.at[q, h, side])
+            across(q, which, h).start()
+        landed(spot(source[q], q, 2, h), yf_send.at[q, h], yf_recv.at[q, h])
+        across(q, 2, h).start()
 
     def whole(q):
         for which in range(NY):
@@ -175,7 +175,7 @@
                 ref = feats.at[
                     source[q],
                     pl.ds(pl.multiple_of((1 - c) * rows + h * half, half), half),
-                    pl.ds(pl.multiple_of(((y + which) % NY) * piece, 128), piece),
+                    pl.ds(pl.multiple_of(((label[q] + which) % NY) * piece, 128), piece),
                 ]
                 landed(ref, dd_send.at[q, which, h], dd_recv.at[q, which, h])
 
@@ -196,7 +196,7 @@
 
     for h in sides:
         for q in sides:
-            landed(spot(source[q], 0, h), xn_send.at[q, h], xn_recv.at[q, h])
+            landed(spot(source[q], q, 0, h), xn_send.at[q, h], xn_recv.at[q, h])
             begin(q, h)
     for side in sides:
         x_far(side).wait_recv()
@@ -207,10 +207,8 @@
         for q in sides:
             middle(q, h)
     for side in sides:
-        landed(spot(far, 0, side), xg_send.at[side], xg_recv.at[side])
+        landed(spot(far, 2, 0, side), xg_send.at[side], xg_recv.at[side])
         begin(2, side)
-    for q in sides:
-        finish(q)
     for q in sides:
         whole(q)
     for copy in local_w:
@@ -261,7 +259,6 @@
     lax.fori_loop(0, chunks, direct, 0)
     for h in sides:
         middle(2, h)
-    finish(2)
     whole(2)
 
     def first(k, carry):
@@ -411,9 +408,9 @@
             x_near(side, h).wait_send()
     for q in range(3):
         for side in sides:
-            y_pass(q, side).wait_send()
+            two(q, side).wait_send()
             for h in sides:
-                y_own(q, h, side).wait_send()
+                one(q, h, side).wait_send()
         for which in range(NY):
             for h in sides:
                 across(q, which, h).wait_send()

time: 163 us -> 149 us (0.914)
  Pallas kernels: 160 us -> 146 us
    pallas_call x2, Pallas kernels: 160 us -> 146 us  [run(): pl.pallas_call(functools.partial(kernel, nx, nz, chunks, exact), out_shap...]
where the time goes in v3:
time: 149 us; the launch traced here: 148 us
  Pallas kernels  146 us (98%)
    pallas_call x2, Pallas kernels, run(): pl.pallas_call(functools.partial(kernel, nx, nz, chunks, exact), out_shap...  146 us

profile of v3, /device:TPU:1, one launch (start us, length us, event | category | flops | bytes accessed | tf_op | source)
XLA Modules:
  0.0 148.4 jit_solution(8166128534738174180)
XLA Ops:
  0.6 0.0 copy-start.4
  0.6 0.0 copy-start.3
  0.7 0.0 copy-start.2
  0.7 0.0 copy-start.1
  0.7 0.0 copy-start
  0.7 64.4 %shard_map.77 = (f32[1,128]{1,0:T(1,128)S(1)}, f32[1,32]{1,0:T(1,128)S(1)}, f32[1,128]{1,0:T(1,128)}) custom-call(bf16[128,8192]{1,0:T(8,128)(2,1)} %hid.1, bf16[1024,3072]{1,0:T(8,128)(2,1)} %w.1, s32[1,128]{1,0:T(1,128)} %bitcast.14, s32[1,128]{1,0:T(1,128)} %bitcast.16, s32[1,128]{1,0:T(1,128)} %bitcast.18, s32[1,32]{1,0:T(1,128)} %bitcast.20), custom_call_target="tpu_custom_call" | custom-call | tf_op jit(solution)/shard_map/pallas_call | solution.py:446
  65.7 0.0 copy-done.4
  65.7 0.0 copy-done.3
  65.7 0.0 copy-done.2
  65.7 0.0 copy-done.1
  65.7 0.0 copy-done
  65.8 81.6 %conditional.1 = (f32[128]{0:T(128)S(1)}, f32[32]{0:T(128)S(1)}) conditional(s32[]{:T(128)} %bitcast.12, (f32[1,128]{1,0:T(1,128)S(1)}, f32[1,32]{1,0:T(1,128)S(1)}) %tuple.30, (s32[128]{0:T(128)S(1)}, s32[128]{0:T(128)S(1)}, s32[128]{0:T(128)S(1)}, s32[32]{0:T(128)S(1)}, bf16[128,8192]{1,0:T(8,128)(2,1)S(1)}, ...), branch_computations={%region_0.0_spmd, %region_1.0_spmd} | conditional | bytes 16 | solution.py:487
  65.8 81.6 %branch_1_fun.1 = (f32[1,128]{1,0:T(1,128)S(1)}, f32[1,32]{1,0:T(1,128)S(1)}, f32[1,128]{1,0:T(1,128)}) custom-call(bf16[128,8192]{1,0:T(8,128)(2,1)S(1)} %get-tuple-element.22.hid, bf16[1024,3072]{1,0:T(8,128)(2,1)} %get-tuple-element.23.w, s32[1,128]{1,0:T(1,128)S(1)} %bitcast.15, s32[1,128]{1,0:T(1,128)S(1)} %bitcast.17, s32[1,128]{1,0:T(1,128)S(1)} %bitcast.19, ...), custom_call_target="tpu_custom_call" | custom-call | tf_op jit(solution)/shard_map/cond/branch_1_fun/pallas_call | solution.py:446
  147.4 0.5 copy.16
  147.9 0.5 copy.17
Async XLA Ops:
  0.6 65.1 %copy-start.4 = (s32[32]{0:T(128)S(1)}, s32[32]{0:T(128)}, u32[]{:S(2)}) copy-start(s32[32]{0:T(128)} %param.13) | copy-start | bytes 388
  0.6 65.1 %copy-start.3 = (s32[128]{0:T(128)S(1)}, s32[128]{0:T(128)}, u32[]{:S(2)}) copy-start(s32[128]{0:T(128)} %param.12) | copy-start | bytes 1540
  0.7 65.1 %copy-start.2 = (s32[128]{0:T(128)S(1)}, s32[128]{0:T(128)}, u32[]{:S(2)}) copy-start(s32[128]{0:T(128)} %param.11) | copy-start | bytes 1540
  0.7 65.1 %copy-start.1 = (s32[128]{0:T(128)S(1)}, s32[128]{0:T(128)}, u32[]{:S(2)}) copy-start(s32[128]{0:T(128)} %param.10) | copy-start | bytes 1540
  0.7 65.1 %copy-start = (bf16[128,8192]{1,0:T(8,128)(2,1)S(1)}, bf16[128,8192]{1,0:T(8,128)(2,1)}, u32[]{:S(2)}) copy-start(bf16[128,8192]{1,0:T(8,128)(2,1)} %hid.1) | copy-start | bytes 6291460
